TPU v7x, 32 devices: a whole 2x2x4 slice. The times are simulated.
32 devices in a mesh: seq: 8 (over z, core), head: 4 (over y, x).
Axes of the slice: x: 2, y: 2, z: 4, core: 2. Of those that a mesh axis runs over, the one named last changes fastest.
Arguments:
- tokens: bfloat16 [1024, 4096], P('seq', 'head'), may hold values from -6 to 6
- w_query: bfloat16 [4096, 4096], P(None, 'head'), may hold values from -0.09375 to 0.09375
- w_key: bfloat16 [4096, 4096], P(None, 'head'), may hold values from -0.09375 to 0.09375
- w_value: bfloat16 [4096, 4096], P(None, 'head'), may hold values from -0.09375 to 0.09375
- upstream: bfloat16 [1024, 4096], P('seq', 'head'), may hold values from -6 to 6
- log_decay: float32 [1024, 32], P('seq', 'head'), may hold values from -1 to 0, as said below
- segment: int32 [1024], replicated, may hold values from 0 to 7, never falling along the last dimension, each value on 1 to 256 neighbouring positions
Outputs:
- grad_query: bfloat16 [4096, 4096], P('seq', 'head')
- grad_key: bfloat16 [4096, 4096], P('seq', 'head')
- grad_value: bfloat16 [4096, 4096], P('seq', 'head')
Inputs may be any that keep to these rules, and one draw needn't show every extreme that they name: log_decay is negative. `segment`: document ids never fall along the tokens; each document holds 1 to 256 tokens.
All inputs are finite; a program needn't handle non-finite values.
Results may differ from a plain program's by a relative error of at most 0.02.
Values may be sent and summed in bfloat16 or wider, within the bound.
A program may use at most 64 MiB of HBM per device.

v0:
```python
import functools

import jax
import jax.numpy as jnp
from jax import lax
from jax.experimental import pallas as pl
from jax.experimental.pallas import tpu as pltpu
from jax.sharding import PartitionSpec as P

HEAD = 128
SCALE = HEAD ** (-0.5)
MESH = pl.DeviceIdType.MESH
VMEM_BYTES = 56 * 1024 * 1024


def dot(a, b, contract=((1,), (0,))):
    return lax.dot_general(a, b, (contract, ((), ())), preferred_element_type=jnp.float32)


def half(x):
    return x.astype(jnp.bfloat16)


def aligned(index, size):
    return pl.ds(pl.multiple_of(index * size, size), size)


def kernel(nz, nh, heads, reach, tok_ref, up_ref, dec_ref, seg_ref, wq_ref, wk_ref, wv_ref, oq_ref, ok_ref, ov_ref, T, U, L, W, q_s, k_s, v_s, acc, D, IN, OUT, CR, LT, R, A, TT, G, zs, zr, uas, uar, ubs, ubr, xs, xr, ds, dr, ps, pr, qs, qr, es, er, ls, lr, own, wsem):
    s, h = lax.axis_index("seq"), lax.axis_index("head")
    z, c = s // 2, s % 2
    nb = 2 * nz
    rows, feat = tok_ref.shape
    width = heads * HEAD
    mate = z * 2 + 1 - c
    relay = nh == 4
    parts = 2 if relay else 1
    piece = feat // parts
    span = (reach + 1) // 2
    lag = max(span, nz - 3)

    def flip(a):
        hi, lo = h // 2, h % 2
        hi = 1 - hi if a // 2 else hi
        lo = 1 - lo if a % 2 else lo
        return hi * 2 + lo

    others = [flip(a) for a in (1, 2, 3)] if relay else [lax.rem(h + a, nh) for a in range(1, nh)]
    sides = 2 if relay else nh - 1
    barrier = pltpu.get_barrier_semaphore()
    targets = [(lax.rem(s + k, nb), h) for k in range(1, nb)] + [(s, o) for o in others]
    for target in targets:
        pl.semaphore_signal(barrier, inc=1, device_id=target, device_id_type=MESH)

    lower = z * 2 < nz
    near = jnp.where(lower, z, nz - 1 - z)

    def turned(pos):
        return jnp.where(lower, pos, nz - 1 - pos)

    def order(p):
        step = (p + 1) // 2
        pos = jnp.where(p > 2 * near, p, jnp.where(p % 2 == 1, near - step, near + step))
        return turned(pos)

    def place(zz, cc, hh, lo=0, size=feat):
        return T.at[aligned(zz * 2 + cc, rows), pl.ds(pl.multiple_of(hh * feat + lo, 128), size)]

    def uplace(zz, cc):
        return U.at[aligned(zz * 2 + cc, rows), :]

    def remote(src, dst, ss, rs, target):
        return pltpu.make_async_remote_copy(src_ref=src, dst_ref=dst, send_sem=ss, recv_sem=rs, device_id=target, device_id_type=MESH)

    my_up = up_ref.at[:, aligned(c, width)]
    their_up = up_ref.at[:, aligned(1 - c, width)]
    stays = [
        pltpu.make_async_copy(tok_ref, place(z, c, h), own.at[0]),
        pltpu.make_async_copy(my_up, uplace(z, c), own.at[1]),
        pltpu.make_async_copy(dec_ref, L.at[s], own.at[2]),
    ]

    def weight(hh):
        at = aligned(hh, feat)
        return [
            pltpu.make_async_copy(w_ref.at[at, aligned(c, width)], W.at[n, at, :], wsem.at[hh, n])
            for n, w_ref in enumerate((wq_ref, wk_ref, wv_ref))
        ]

    everyone = [h] + others
    for copy in stays:
        copy.start()
    for hh in everyone:
        for copy in weight(hh):
            copy.start()

    def z_copy(src, zz, up):
        to = (z + 1 if up else z - 1) * 2 + c
        return remote(src, place(zz, c, h), zs.at[up, zz], zr.at[zz], (to, h))

    def ua_copy(src, zz, up):
        to = (z + 1 if up else z - 1) * 2 + c
        return remote(src, uplace(zz, c), uas.at[up, zz], uar.at[zz], (to, h))

    def ub_copy(zz, up):
        to = (z + 1 if up else z - 1) * 2 + c
        return remote(uplace(zz, 1 - c), uplace(zz, 1 - c), ubs.at[up, zz], ubr.at[zz], (to, h))

    def side_copy(src, zz, j, n):
        lo = n * piece
        return remote(src.at[:, pl.ds(lo, piece)], place(zz, c, h, lo, piece), xs.at[j, n, zz], xr.at[j, n, zz], (s, others[j]))

    def side_arrival(zz, j, n):
        here = place(zz, c, others[j], n * piece, piece)
        return remote(here, here, xs.at[j, n, zz], xr.at[j if relay else nh - 2 - j, n, zz], (mate, h))

    def diag_copy(zz, j):
        part = place(zz, c, others[j], j * piece, piece)
        return remote(part, part, ds.at[j, zz], dr.at[j, zz], (s, others[1 - j]))

    def diag_arrival(zz, j):
        part = place(zz, c, others[2], j * piece, piece)
        return remote(part, part, ds.at[j, zz], dr.at[j, zz], (mate, h))

    def mate_copy(src, zz, hh):
        return remote(src, place(zz, c, hh), ps.at[zz, hh], pr.at[zz, hh], (mate, h))

    def mate_arrival(zz, hh):
        there = place(zz, 1 - c, hh)
        return remote(there, there, ps.at[zz, hh], pr.at[zz, hh], (mate, h))

    def swap(b):
        return remote(A.at[0, aligned(b, rows)], A.at[1, aligned(b, rows)], es.at[b], er.at[b], (mate, h))

    mate_up = remote(their_up, uplace(z, c), qs.at[0], qr.at[0], (mate, h))
    small = [remote(dec_ref, L.at[s], ls.at[k], lr.at[k], (lax.rem(s + k, nb), h)) for k in range(1, nb)]

    def spread(src, zz):
        for j in range(sides):
            side_copy(src, zz, j, j if relay else 0).start()
        if relay:
            for j in range(sides):
                side_copy(src, zz, j, 1 - j).start()
        mate_copy(src, zz, h).start()

    goes_up, goes_down = z + 1 < nz, z >= 1

    def along(zz, what):
        @pl.when((zz <= z) & goes_up)
        def _():
            what(1)

        @pl.when((zz >= z) & goes_down)
        def _():
            what(0)

    def each(k, what):
        @pl.when(z - k >= 0)
        def _():
            what(z - k)

        @pl.when(z + k < nz)
        def _():
            what(z + k)

    def passed(zz):
        return ((zz < z) & goes_up) | ((zz > z) & goes_down)

    def take_z(k):
        def one(zz):
            here = place(zz, c, h)
            z_copy(here, zz, 0).wait_recv()

            def forward(up):
                z_copy(here, zz, up).start()

                @pl.when(k == 1)
                def _():
                    ub_copy(z, up).start()

            along(zz, forward)

        each(k, one)

    def wait_u(zz):
        ua_copy(uplace(zz, c), zz, 0).wait_recv()
        ub_copy(zz, 0).wait_recv()

    def pass_u(zz):
        @pl.when(passed(zz))
        def _():
            wait_u(zz)

            def forward(up):
                ua_copy(uplace(zz, c), zz, up).start()
                ub_copy(zz, up).start()

            along(zz, forward)

    pl.semaphore_wait(barrier, len(targets))
    for copy in small:
        copy.start()
    along(z, lambda up: z_copy(tok_ref, z, up).start())
    spread(tok_ref, z)
    mate_up.start()
    along(z, lambda up: ua_copy(my_up, z, up).start())

    i = lax.broadcasted_iota(jnp.int32, (rows, rows), 0)
    j = lax.broadcasted_iota(jnp.int32, (rows, rows), 1)

    def wide(row):
        return jnp.broadcast_to(row, (rows, rows))

    zero = jnp.zeros((HEAD, HEAD), jnp.float32)
    for a in range(heads):
        for n in range(reach):
            for at in (n, nb + reach + n):
                LT[a, at] = zero
                R[a, at] = zero
                CR[a, at] = zero[:8]

    def clear(n, _):
        G[:, aligned(n, 8), :] = jnp.zeros((2, 8, G.shape[2]), jnp.float32)
        return 0

    lax.fori_loop(0, G.shape[1] // 8, clear, 0)
    for copy in stays:
        copy.wait()
    there = uplace(z, 1 - c)
    remote(there, there, qs.at[0], qr.at[0], (mate, h)).wait_recv()

    @pl.when(goes_up & (z == 0))
    def _():
        ub_copy(z, 1).start()

    @pl.when(goes_down & (z == nz - 1))
    def _():
        ub_copy(z, 0).start()

    for k in range(1, nb):
        there = L.at[lax.rem(s + nb - k, nb)]
        remote(there, there, ls.at[k], lr.at[k], (mate, h)).wait_recv()
    triangle = jnp.where(i <= j, 1.0, 0.0).astype(jnp.float32)
    L[...] = lax.dot_general(
        L[...].reshape(nb * L.shape[1], rows), triangle, (((1,), (0,)), ((), ())), precision=lax.Precision.HIGHEST, preferred_element_type=jnp.float32
    ).reshape(L.shape)

    def tables(b, _):
        segs = wide(seg_ref[pl.ds(b, 1), :].astype(jnp.float32))
        ahead = seg_ref[pl.ds(jnp.maximum(b - 1, 0), 1), rows - 1 :].astype(jnp.float32)
        before = wide(jnp.where(b == 0, -1.0, ahead))
        segs_down = segs.T
        last_seg = wide(segs[:1, rows - 1 :])
        same = (segs == segs_down) & (i >= j)
        for a in range(heads):
            ahead_sum = wide(L[b, pl.ds(c * heads + a, 1), :])
            down = ahead_sum.T
            last = wide(ahead_sum[:1, rows - 1 :])
            D[a, b] = jnp.where(same, SCALE * jnp.exp(jnp.where(same, down - ahead_sum, 0.0)), 0.0)
            IN[a, b] = jnp.where(segs_down == before, jnp.exp(down), 0.0)
            OUT[a, b] = jnp.where(segs_down == last_seg, jnp.exp(last - down), 0.0)
            CR[a, b + reach] = jnp.where(last_seg == before, jnp.exp(last), 0.0)[:8]
        return 0

    lax.fori_loop(0, nb, tables, 0)

    def pair(zz):
        return aligned(zz, 2 * rows)

    def project(zz, hh, first, done):
        mate_arrival(zz, hh).wait_recv()
        x = T[pair(zz), aligned(hh, feat)]
        for n, out in enumerate((q_s, k_s, v_s)):
            new = dot(x, W[n, aligned(hh, feat), :])
            cols = slice(n * width, (n + 1) * width)
            if not first:
                new = acc[:, cols] + new
            if done:
                out[pair(zz), :] = half(new)
            else:
                acc[:, cols] = new

    def cols(a):
        return slice(a * HEAD, (a + 1) * HEAD)

    def states(zz):
        def block(n, _):
            b = zz * 2 + n
            at = aligned(b, rows)
            for a in range(heads):
                weighted_k = half(OUT[a, b] * k_s[at, cols(a)].astype(jnp.float32))
                weighted_q = half(IN[a, b] * q_s[at, cols(a)].astype(jnp.float32))
                LT[a, b + reach] = dot(v_s[at, cols(a)], weighted_k, ((0,), (0,)))
                R[a, b + reach] = dot(weighted_q, U[at, cols(a)], ((0,), (0,)))
            return 0

        lax.fori_loop(0, 2, block, 0)

    def attend(zz):
        def block(n, _):
            b = zz * 2 + n
            at = aligned(b, rows)
            for a in range(heads):
                q, k, v, u = q_s[at, cols(a)], k_s[at, cols(a)], v_s[at, cols(a)], U[at, cols(a)]
                coming, back = LT[a, b], R[a, b + 2 * reach]
                for m in range(reach - 1, 0, -1):
                    coming = wide(CR[a, b + reach - m, :1]) * coming + LT[a, b + reach - m]
                    back = wide(CR[a, b + reach + m, :1]) * back + R[a, b + reach + m]
                coming, back = half(SCALE * coming), half(SCALE * back)
                decay, inflow, outflow = D[a, b], IN[a, b], OUT[a, b]
                attn_qk = half(decay * dot(q, k, ((1,), (1,))))
                attn_up = half(decay * dot(u, v, ((1,), (1,))))
                in_u = half(inflow * u.astype(jnp.float32))
                out_v = half(outflow * v.astype(jnp.float32))
                out_k = half(outflow * k.astype(jnp.float32))
                gq = dot(attn_up, k) + dot(in_u, coming)
                gk = dot(attn_up, q, ((0,), (0,))) + dot(out_v, back, ((1,), (1,)))
                gv = dot(attn_qk, u, ((0,), (0,))) + dot(out_k, back)
                for g, value in enumerate((gq, gk, gv)):
                    A[0, at, g * width + a * HEAD : g * width + (a + 1) * HEAD] = half(value)
            return 0

        lax.fori_loop(0, 2, block, 0)
        swap(zz * 2).start()
        swap(zz * 2 + 1).start()

    depth_rows = TT.shape[0]

    def turn(zz):
        TT[:, pair(zz)] = T[pair(zz), aligned(s, depth_rows)].T

    def gather(zz):
        swap(zz * 2).wait_recv()
        swap(zz * 2 + 1).wait_recv()
        for slot in range(2):
            for g in range(3):
                at = slice(g * width, (g + 1) * width)
                G[slot, :, at] += dot(TT[:, pair(zz)], A[slot, pair(zz), at])

    def step(p, _):
        zz = order(p)
        live = p < nz

        @pl.when(live)
        def _():
            for n in range(sides):
                side_arrival(zz, n, n if relay else 0).wait_recv()
                if relay:
                    diag_copy(zz, n).start()
                else:
                    mate_copy(place(zz, c, others[n]), zz, others[n]).start()

        @pl.when(p == 2)
        def _():
            each(1, pass_u)

        @pl.when((p >= 1) & (p <= nz))
        def _():
            old = order(p - 1)
            if relay:
                project(old, others[2], False, True)

            @pl.when((old != z) & jnp.logical_not(passed(old)))
            def _():
                wait_u(old)

            states(old)
            turn(old)

        @pl.when(live)
        def _():
            @pl.when(p == 0)
            def _():
                for copy in weight(h):
                    copy.wait()

            project(zz, h, True, False)

        @pl.when(p + 1 < nz)
        def _():
            take_z(p + 1)
            later = order(p + 1)
            spread(place(later, c, h), later)

        @pl.when((p >= 2) & (p < nz))
        def _():
            each(p, pass_u)

        if relay:
            @pl.when(live)
            def _():
                for n in range(sides):
                    side_arrival(zz, n, 1 - n).wait_recv()
                    mate_copy(place(zz, c, others[n]), zz, others[n]).start()

        @pl.when(p >= lag + 1)
        def _():
            attend(turned(p - lag - 1))

        @pl.when(live)
        def _():
            if relay:
                far = others[2]
                for n in range(2):
                    diag_arrival(zz, n).wait_recv()
                mate_copy(place(zz, c, far), zz, far).start()

            @pl.when(p == 0)
            def _():
                for hh in others:
                    for copy in weight(hh):
                        copy.wait()

            for n in range(sides):
                project(zz, others[n], False, (not relay) and n == sides - 1)

            @pl.when(p >= lag + 1)
            def _():
                gather(turned(p - lag - 1))

        return 0

    lax.fori_loop(0, nz + lag + 1, step, 0)
    lax.fori_loop(nz - lag - 1 if nz > lag else 0, nz - 1, lambda a, _: (gather(turned(a)), 0)[1], 0)

    final = turned(nz - 1)
    for slot in range(2):
        if slot == 1:
            swap(final * 2).wait_recv()
            swap(final * 2 + 1).wait_recv()
        put = aligned(c if slot == 0 else 1 - c, width)
        for g, out in enumerate((oq_ref, ok_ref, ov_ref)):
            at = slice(g * width, (g + 1) * width)
            out[:, put] = half(G[slot, :, at] + dot(TT[:, pair(final)], A[slot, pair(final), at]))

    def drain(zz, _):
        here = place(zz, c, h)

        def sent(up):
            z_copy(here, zz, up).wait_send()
            ua_copy(uplace(zz, c), zz, up).wait_send()
            ub_copy(zz, up).wait_send()

        along(zz, sent)
        for n in range(sides):
            for m in range(parts):
                side_copy(here, zz, n, m).wait_send()
        if relay:
            for n in range(2):
                diag_copy(zz, n).wait_send()
        for hh in everyone:
            mate_copy(place(zz, c, hh), zz, hh).wait_send()
        swap(zz * 2).wait_send()
        swap(zz * 2 + 1).wait_send()
        return 0

    lax.fori_loop(0, nz, drain, 0)
    mate_up.wait_send()
    for copy in small:
        copy.wait_send()


def local(n_seq, nh, tokens, w_query, w_key, w_value, upstream, log_decay, segment):
    nz = n_seq // 2
    rows, feat = tokens.shape
    total, depth = rows * n_seq, feat * nh
    heads = w_query.shape[1] // HEAD // 2
    width = heads * HEAD
    reach = total // 4 // rows
    parts = 2 if nh == 4 else 1
    decay = jnp.zeros((max(8, 2 * heads), rows), jnp.float32).at[: 2 * heads].set(log_decay.T)
    seg = segment.reshape(n_seq, rows)
    kind = tokens.dtype
    dma = pltpu.SemaphoreType.DMA
    vmem = pl.BlockSpec(memory_space=pltpu.VMEM)
    hbm = pl.BlockSpec(memory_space=pl.ANY)
    f32 = jnp.float32
    square = (HEAD, HEAD)
    padded = n_seq + 2 * reach
    out_rows = depth // n_seq
    return tuple(pl.pallas_call(
        functools.partial(kernel, nz, nh, heads, reach),
        out_shape=[pltpu.VMEM((out_rows, 2 * width), kind)] * 3,
        in_specs=[vmem] * 4 + [hbm] * 3,
        out_specs=[vmem] * 3,
        scratch_shapes=[
            pltpu.VMEM((total, depth), kind),
            pltpu.VMEM((total, width), kind),
            pltpu.VMEM((n_seq,) + decay.shape, f32),
            pltpu.VMEM((3, depth, width), kind),
        ]
        + [pltpu.VMEM((total, width), kind)] * 3
        + [pltpu.VMEM((2 * rows, 3 * width), f32)]
        + [pltpu.VMEM((heads, n_seq) + square, f32)] * 3
        + [pltpu.VMEM((heads, padded, 8, HEAD), f32)]
        + [pltpu.VMEM((heads, padded) + square, f32)] * 2
        + [
            pltpu.VMEM((2, total, 3 * width), kind),
            pltpu.VMEM((out_rows, total), kind),
            pltpu.VMEM((2, out_rows, 3 * width), f32),
        ]
        + [dma((2, nz)), dma((nz,))] * 3
        + [dma((nh - 1, parts, nz))] * 2
        + [dma((2, nz))] * 2
        + [dma((nz, nh))] * 2
        + [dma((1,))] * 2
        + [dma((n_seq,))] * 4
        + [dma((3,)), dma((nh, 3))],
        compiler_params=pltpu.CompilerParams(collective_id=0, has_side_effects=True, vmem_limit_bytes=VMEM_BYTES),
    )(tokens, upstream, decay, seg, w_query, w_key, w_value))


def solution(mesh):
    placed = (P("seq", "head"), P(None, "head"), P(None, "head"), P(None, "head"), P("seq", "head"), P("seq", "head"), P())
    return jax.shard_map(
        functools.partial(local, mesh.shape["seq"], mesh.shape["head"]),
        mesh=mesh,
        in_specs=placed,
        out_specs=(P("seq", "head"),) * 3,
        check_vma=False,
    )
```

profile of v0, /device:TPU:9, one launch (start us, length us, event | category | flops | bytes accessed | tf_op | source)
XLA Modules:
  0.0 60.7 jit_solution(4085823392358979613)
XLA Ops:
  0.6 57.1 %shard_map.99 = (bf16[512,1024]{1,0:T(8,128)(2,1)S(1)}, bf16[512,1024]{1,0:T(8,128)(2,1)S(1)}, bf16[512,1024]{1,0:T(8,128)(2,1)S(1)}) custom-call(bf16[128,1024]{1,0:T(8,128)(2,1)} %tok_ref.1, bf16[128,1024]{1,0:T(8,128)(2,1)} %up_ref.1, f32[8,128]{1,0:T(8,128)} %bitcast.2, s32[8,128]{1,0:T(8,128)} %bitcast.3, bf16[4096,1024]{1,0:T(8,128)(2,1)} %wq_ref.1, ...), custom_call_target="tpu_custom_call" | custom-call | tf_op jit(solution)/shard_map/pallas_call | solution.py:480
  57.8 1.0 %copy.13 = bf16[512,1024]{1,0:T(8,128)(2,1)} copy(bf16[512,1024]{1,0:T(8,128)(2,1)S(1)} %get-tuple-element.23) | data formatting | bytes 2097152
  58.7 1.0 %copy.14 = bf16[512,1024]{1,0:T(8,128)(2,1)} copy(bf16[512,1024]{1,0:T(8,128)(2,1)S(1)} %get-tuple-element.24) | data formatting | bytes 2097152
  59.7 1.0 %copy.15 = bf16[512,1024]{1,0:T(8,128)(2,1)} copy(bf16[512,1024]{1,0:T(8,128)(2,1)S(1)} %get-tuple-element.25) | data formatting | bytes 2097152
where the time goes:
time: 60.8 us; the launch traced here: 60.7 us
  Pallas kernels  57.1 us (94%)
  local copies, waits for them, and re-layouts  2.91 us (5%)
  between operations  0.64 us (1%)
    pallas_call x1, Pallas kernels, local(): pl.pallas_call(functools.partial(kernel, nz, nh, heads, reach), out_shape...  57.1 us
    unnamed x3, local copies, waits for them, and re-layouts  2.91 us

commit v1 on v0

v1 whole, which is shorter than its diff:
```python
import functools

import jax
import jax.numpy as jnp
from jax import lax
from jax.experimental import pallas as pl
from jax.experimental.pallas import tpu as pltpu
from jax.sharding import PartitionSpec as P

HEAD = 128
SCALE = HEAD ** (-0.5)
MESH = pl.DeviceIdType.MESH
VMEM_BYTES = 57 * 1024 * 1024


def dot(a, b, contract=((1,), (0,))):
    return lax.dot_general(a, b, (contract, ((), ())), preferred_element_type=jnp.float32)


def half(x):
    return x.astype(jnp.bfloat16)


def whole(x):
    return x.astype(jnp.float32)


def aligned(index, size):
    return pl.ds(pl.multiple_of(index * size, size), size)


def kernel(nz, nh, heads, reach, tok_ref, up_ref, dec_ref, seg_in, wq_ref, wk_ref, wv_ref, oq_ref, ok_ref, ov_ref, T, U, L, seg_ref, W, q_s, k_s, v_s, acc, D, IN, OUT, CR, LT, R, A, B, TT, G, zs, zr, uas, uar, ubs, ubr, xs, xr, ds, dr, ps, pr, qs, qr, es, er, es2, er2, ls, lr, own, wsem):
    s, h = lax.axis_index("seq"), lax.axis_index("head")
    z, c = s // 2, s % 2
    nb = 2 * nz
    rows, feat = tok_ref.shape
    width = heads * HEAD
    mate = z * 2 + 1 - c
    relay = nh == 4
    parts = 2 if relay else 1
    piece = feat // parts
    span = (reach + 1) // 2
    lag = max(span, nz - 3)
    slots = B.shape[0] // (2 * rows)

    def flip(a):
        hi, lo = h // 2, h % 2
        hi = 1 - hi if a // 2 else hi
        lo = 1 - lo if a % 2 else lo
        return hi * 2 + lo

    others = [flip(a) for a in (1, 2, 3)] if relay else [lax.rem(h + a, nh) for a in range(1, nh)]
    sides = 2 if relay else nh - 1
    barrier = pltpu.get_barrier_semaphore()
    goes_up, goes_down = z + 1 < nz, z >= 1
    for target in [(mate, h)] + [(s, o) for o in others]:
        pl.semaphore_signal(barrier, inc=1, device_id=target, device_id_type=MESH)

    @pl.when(goes_up)
    def _():
        pl.semaphore_signal(barrier, inc=1, device_id=(s + 2, h), device_id_type=MESH)

    @pl.when(goes_down)
    def _():
        pl.semaphore_signal(barrier, inc=1, device_id=(s - 2, h), device_id_type=MESH)

    lower = z * 2 < nz
    near = jnp.where(lower, z, nz - 1 - z)

    def turned(pos):
        return jnp.where(lower, pos, nz - 1 - pos)

    def order(p):
        step = (p + 1) // 2
        pos = jnp.where(p > 2 * near, p, jnp.where(p % 2 == 1, near - step, near + step))
        return turned(pos)

    def place(zz, cc, hh, lo=0, size=feat):
        return T.at[aligned(zz * 2 + cc, rows), pl.ds(pl.multiple_of(hh * feat + lo, 128), size)]

    def uplace(zz, cc):
        return U.at[aligned(zz * 2 + cc, rows), :]

    def remote(src, dst, ss, rs, target):
        return pltpu.make_async_remote_copy(src_ref=src, dst_ref=dst, send_sem=ss, recv_sem=rs, device_id=target, device_id_type=MESH)

    my_up = up_ref.at[:, aligned(c, width)]
    their_up = up_ref.at[:, aligned(1 - c, width)]
    stays = [
        pltpu.make_async_copy(tok_ref, place(z, c, h), own.at[0]),
        pltpu.make_async_copy(my_up, uplace(z, c), own.at[1]),
        pltpu.make_async_copy(dec_ref, L.at[s], own.at[2]),
        pltpu.make_async_copy(seg_in, seg_ref, own.at[3]),
    ]

    def weight(hh):
        at = aligned(hh, feat)
        return [
            pltpu.make_async_copy(w_ref.at[at, aligned(c, width)], W.at[at, pl.ds(n * width, width)], wsem.at[hh, n])
            for n, w_ref in enumerate((wq_ref, wk_ref, wv_ref))
        ]

    everyone = [h] + others
    for copy in stays + weight(h):
        copy.start()

    def z_copy(src, zz, up):
        to = (z + 1 if up else z - 1) * 2 + c
        return remote(src, place(zz, c, h), zs.at[up, zz], zr.at[zz], (to, h))

    def ua_copy(src, zz, up):
        to = (z + 1 if up else z - 1) * 2 + c
        return remote(src, uplace(zz, c), uas.at[up, zz], uar.at[zz], (to, h))

    def ub_copy(zz, up):
        to = (z + 1 if up else z - 1) * 2 + c
        return remote(uplace(zz, 1 - c), uplace(zz, 1 - c), ubs.at[up, zz], ubr.at[zz], (to, h))

    def side_copy(src, zz, j, n):
        lo = n * piece
        return remote(src.at[:, pl.ds(lo, piece)], place(zz, c, h, lo, piece), xs.at[j, n, zz], xr.at[j, n, zz], (s, others[j]))

    def side_arrival(zz, j, n):
        here = place(zz, c, others[j], n * piece, piece)
        return remote(here, here, xs.at[j, n, zz], xr.at[j if relay else nh - 2 - j, n, zz], (mate, h))

    def diag_copy(zz, j):
        part = place(zz, c, others[j], j * piece, piece)
        return remote(part, part, ds.at[j, zz], dr.at[j, zz], (s, others[1 - j]))

    def diag_arrival(zz, j):
        part = place(zz, c, others[2], j * piece, piece)
        return remote(part, part, ds.at[j, zz], dr.at[j, zz], (mate, h))

    def mate_copy(zz, hh, n=0, size=feat):
        here = place(zz, c, hh, n * piece, size)
        return remote(here, here, ps.at[zz, hh, n], pr.at[zz, hh, n], (mate, h))

    def mate_arrival(zz, hh, n=0, size=feat):
        there = place(zz, 1 - c, hh, n * piece, size)
        return remote(there, there, ps.at[zz, hh, n], pr.at[zz, hh, n], (mate, h))

    def swap(b):
        return remote(A.at[0, aligned(b, rows)], A.at[1, aligned(b, rows)], es.at[b], er.at[b], (mate, h))

    mate_up = remote(their_up, uplace(z, c), qs.at[0], qr.at[0], (mate, h))

    def l_copy(zz, up):
        to = (z + 1 if up else z - 1) * 2 + c
        here = L.at[zz * 2 + c]
        return remote(here, here, ls.at[up, zz], lr.at[zz], (to, h))

    def l_mate(zz, cc):
        here = L.at[zz * 2 + cc]
        return remote(here, here, es2.at[zz], er2.at[zz], (mate, h))

    def spread(src, zz):
        for j in range(sides):
            side_copy(src, zz, j, j if relay else 0).start()
        if relay:
            for j in range(sides):
                side_copy(src, zz, j, 1 - j).start()
        mate_copy(zz, h).start()

    def along(zz, what):
        @pl.when((zz <= z) & goes_up)
        def _():
            what(1)

        @pl.when((zz >= z) & goes_down)
        def _():
            what(0)

    def each(k, what):
        for zz in (jnp.where(lower, z - k, z + k), jnp.where(lower, z + k, z - k)):
            pl.when((zz >= 0) & (zz < nz))(functools.partial(what, zz))

    def outer(zz):
        return (zz == 0) | (zz == nz - 1)

    def passed(zz):
        return ((zz < z) & goes_up) | ((zz > z) & goes_down)

    def take_z(k):
        def one(zz):
            here = place(zz, c, h)
            l_copy(zz, 0).wait_recv()
            l_mate(zz, c).start()
            along(zz, lambda up: l_copy(zz, up).start())
            z_copy(here, zz, 0).wait_recv()

            def forward(up):
                z_copy(here, zz, up).start()

                @pl.when(k == 1)
                def _():
                    ub_copy(z, up).start()

            along(zz, forward)
            pl.when(zz == order(k))(lambda: spread(here, zz))

        each(k, one)

    def wait_u(zz):
        ua_copy(uplace(zz, c), zz, 0).wait_recv()
        ub_copy(zz, 0).wait_recv()

    def pass_u(zz):
        @pl.when(passed(zz))
        def _():
            wait_u(zz)

            def forward(up):
                ua_copy(uplace(zz, c), zz, up).start()
                ub_copy(zz, up).start()

            along(zz, forward)

    for copy in stays:
        copy.wait()
    i = lax.broadcasted_iota(jnp.int32, (rows, rows), 0)
    j = lax.broadcasted_iota(jnp.int32, (rows, rows), 1)
    triangle = jnp.where(i <= j, 1.0, 0.0).astype(jnp.float32)
    L[s] = lax.dot_general(L[s], triangle, (((1,), (0,)), ((), ())), precision=lax.Precision.HIGHEST, preferred_element_type=jnp.float32)
    pl.semaphore_wait(barrier, 1 + len(others) + jnp.where(goes_up, 1, 0) + jnp.where(goes_down, 1, 0))
    mine = place(z, c, h)
    l_mate(z, c).start()
    along(z, lambda up: l_copy(z, up).start())
    along(z, lambda up: z_copy(mine, z, up).start())
    spread(mine, z)
    mate_up.start()
    along(z, lambda up: ua_copy(uplace(z, c), z, up).start())
    for hh in others:
        for copy in weight(hh):
            copy.start()

    def wide(row):
        return jnp.broadcast_to(row, (rows, rows))

    def start_up():
        there = uplace(z, 1 - c)
        remote(there, there, qs.at[0], qr.at[0], (mate, h)).wait_recv()

        @pl.when(goes_up & (z == 0))
        def _():
            ub_copy(z, 1).start()

        @pl.when(goes_down & (z == nz - 1))
        def _():
            ub_copy(z, 0).start()


    def pair(zz):
        return aligned(zz, 2 * rows)

    def project(p, hh, first=False, done=False, n=0, size=feat):
        zz, half_way = order(p), acc.at[p % 2]
        mate_arrival(zz, hh, n, size).wait_recv()
        some = pl.ds(pl.multiple_of(hh * feat + n * piece, size), size)
        for m, out in enumerate((q_s, k_s, v_s)):
            pick = slice(m * width, (m + 1) * width)
            new = dot(T[pair(zz), some], W[some, pick])
            if not first:
                new = half_way[:, pick] + new
            if done:
                out[pair(zz), :] = half(new)
            else:
                half_way[:, pick] = new

    def tables(zz):
        l_mate(zz, 1 - c).wait_recv()

        def block(b, _):
            segs = wide(seg_ref[pl.ds(b, 1), :].astype(jnp.float32))
            ahead = seg_ref[pl.ds(jnp.maximum(b - 1, 0), 1), rows - 1 :].astype(jnp.float32)
            before = wide(jnp.where(b == 0, -1.0, ahead))
            segs_down = segs.T
            last_seg = wide(segs[:1, rows - 1 :])
            same = (segs == segs_down) & (i >= j)
            for a in range(heads):
                ahead_sum = wide(L[b, pl.ds(c * heads + a, 1), :])
                down = ahead_sum.T
                last = wide(ahead_sum[:1, rows - 1 :])
                D[a, b] = jnp.where(same, SCALE * jnp.exp(jnp.where(same, down - ahead_sum, 0.0)), 0.0)
                IN[a, b] = jnp.where(segs_down == before, jnp.exp(down), 0.0)
                OUT[a, b] = jnp.where(segs_down == last_seg, jnp.exp(last - down), 0.0)
                CR[a, b + reach] = jnp.where(last_seg == before, jnp.exp(last), 0.0)[:8]
            return 0

        lax.fori_loop(zz * 2, zz * 2 + 2, block, 0)

    def prepare():
        zero = jnp.zeros((HEAD, HEAD), jnp.float32)
        for a in range(heads):
            for n in range(reach):
                for at in (n, nb + reach + n):
                    LT[a, at] = half(zero)
                    R[a, at] = half(zero)
                    CR[a, at] = zero[:8]

        def clear(n, _):
            G[:, aligned(n, 8), :] = jnp.zeros((2, 8, G.shape[2]), jnp.float32)
            return 0

        lax.fori_loop(0, G.shape[1] // 8, clear, 0)
        for copy in weight(h):
            copy.wait()
        project(0, h, first=True)
        tables(z)

    def cols(a):
        return slice(a * HEAD, (a + 1) * HEAD)

    def states(zz):
        for n in range(2):
            b = zz * 2 + n
            at = aligned(b, rows)
            for a in range(heads):
                weighted_k = half(OUT[a, b] * k_s[at, cols(a)].astype(jnp.float32))
                weighted_q = half(IN[a, b] * q_s[at, cols(a)].astype(jnp.float32))
                LT[a, b + reach] = half(dot(v_s[at, cols(a)], weighted_k, ((0,), (0,))))
                R[a, b + reach] = half(dot(weighted_q, U[at, cols(a)], ((0,), (0,))))

    def inside(zz):
        scores = []
        for n in range(2):
            b = zz * 2 + n
            at = aligned(b, rows)
            for a in range(heads):
                decay = D[a, b]
                attn_qk = half(decay * dot(q_s[at, cols(a)], k_s[at, cols(a)], ((1,), (1,))))
                attn_up = half(decay * dot(U[at, cols(a)], v_s[at, cols(a)], ((1,), (1,))))
                scores.append((n, a, attn_qk, attn_up))
        for n, a, attn_qk, attn_up in scores:
            at = aligned(zz * 2 + n, rows)
            put = aligned((zz % slots) * 2 + n, rows)
            B[put, cols(a)] = dot(attn_up, k_s[at, cols(a)])
            B[put, cols(heads + a)] = dot(attn_up, q_s[at, cols(a)], ((0,), (0,)))
            B[put, cols(2 * heads + a)] = dot(attn_qk, U[at, cols(a)], ((0,), (0,)))

    def between(zz):
        for n in range(2):
            b = zz * 2 + n
            at = aligned(b, rows)
            put = aligned((zz % slots) * 2 + n, rows)
            for a in range(heads):
                coming, back = whole(LT[a, b]), whole(R[a, b + 2 * reach])
                for m in range(reach - 1, 0, -1):
                    coming = wide(CR[a, b + reach - m, :1]) * coming + whole(LT[a, b + reach - m])
                    back = wide(CR[a, b + reach + m, :1]) * back + whole(R[a, b + reach + m])
                coming, back = half(SCALE * coming), half(SCALE * back)
                inflow, outflow = IN[a, b], OUT[a, b]
                in_u = half(inflow * U[at, cols(a)].astype(jnp.float32))
                out_v = half(outflow * v_s[at, cols(a)].astype(jnp.float32))
                out_k = half(outflow * k_s[at, cols(a)].astype(jnp.float32))
                terms = (dot(in_u, coming), dot(out_v, back, ((1,), (1,))), dot(out_k, back))
                for g, value in enumerate(terms):
                    A[0, at, cols(g * heads + a)] = half(B[put, cols(g * heads + a)] + value)
            swap(b).start()

    depth_rows = TT.shape[0]

    def turn(zz):
        TT[:, pair(zz)] = T[pair(zz), aligned(s, depth_rows)].T

    def gather(zz):
        swap(zz * 2).wait_recv()
        swap(zz * 2 + 1).wait_recv()
        for slot in range(2):
            for g in range(3):
                pick = slice(g * width, (g + 1) * width)
                G[slot, :, pick] += dot(TT[:, pair(zz)], A[slot, pair(zz), pick])

    prepare()

    def step(p, _):
        zz = order(p)
        live = p < nz

        @pl.when(live)
        def _():
            for n in range(sides):
                side_arrival(zz, n, n if relay else 0).wait_recv()
                if relay:
                    diag_copy(zz, n).start()
                    mate_copy(zz, others[n], n, piece).start()
                else:
                    mate_copy(zz, others[n]).start()

        pl.when(p == 0)(start_up)

        @pl.when(p == 2)
        def _():
            each(1, lambda zz: pl.when(jnp.logical_not(outer(zz)))(lambda: pass_u(zz)))

        @pl.when((p >= 1) & (p <= nz))
        def _():
            old = order(p - 1)

            @pl.when((old != z) & jnp.logical_not(passed(old)))
            def _():
                wait_u(old)

            states(old)
            turn(old)

        @pl.when((p >= 1) & live)
        def _():
            tables(zz)

        @pl.when(p + 1 < nz)
        def _():
            later = order(p + 1)
            pl.when(jnp.abs(later - z) <= p)(lambda: spread(place(later, c, h), later))
            take_z(p + 1)

        @pl.when(p == 1)
        def _():
            each(1, lambda zz: pl.when(outer(zz))(lambda: pass_u(zz)))

        @pl.when((p >= 2) & (p < nz))
        def _():
            each(p, pass_u)

        @pl.when((p >= 1) & (p <= nz))
        def _():
            inside(order(p - 1))

        @pl.when(p == 0)
        def _():
            for hh in others:
                for copy in weight(hh):
                    copy.wait()

        if relay:
            @pl.when(live)
            def _():
                for n in range(sides):
                    side_arrival(zz, n, 1 - n).wait_recv()
                    mate_copy(zz, others[n], 1 - n, piece).start()
                for n in range(sides):
                    project(p, others[n], n=n, size=piece)

        @pl.when(p >= lag + 1)
        def _():
            between(turned(p - lag - 1))

        @pl.when(p + 1 < nz)
        def _():
            project(p + 1, h, first=True)

        @pl.when(live)
        def _():
            if relay:
                def take_diag():
                    for n in range(2):
                        diag_arrival(zz, n).wait_recv()
                    mate_copy(zz, others[2]).start()

                pl.when(p + 1 < nz)(take_diag)
                for n in range(sides):
                    project(p, others[n], n=1 - n, size=piece)
                pl.when(p + 1 == nz)(take_diag)
            else:
                for n in range(sides):
                    project(p, others[n], done=n == sides - 1)

        @pl.when((p >= lag + 1) & live)
        def _():
            gather(turned(p - lag - 1))

        if relay:
            @pl.when(live)
            def _():
                project(p, others[2], done=True)

        return 0

    lax.fori_loop(0, nz + lag + 1, step, 0)
    late = lag + 1
    first = jnp.where(lower, nz - late, 0)
    final = turned(nz - 1)

    def run(start, count):
        return pl.ds(pl.multiple_of(start * 2 * rows, 2 * rows), count * 2 * rows)

    def finish(slot, at):
        put = aligned(c if slot == 0 else 1 - c, width)
        for g, out in enumerate((oq_ref, ok_ref, ov_ref)):
            pick = slice(g * width, (g + 1) * width)
            out[:, put] = half(G[slot, :, pick] + dot(TT[:, at], A[slot, at, pick]))

    finish(0, run(first, late))
    early = jnp.where(lower, nz - late, 1)
    for n in range(2 * late - 2):
        swap(early * 2 + n).wait_recv()
    for g in range(3):
        pick = slice(g * width, (g + 1) * width)
        G[1, :, pick] += dot(TT[:, run(early, late - 1)], A[1, run(early, late - 1), pick])
    for n in range(2):
        swap(final * 2 + n).wait_recv()
    finish(1, pair(final))

    def drain(zz, _):
        here = place(zz, c, h)

        def sent(up):
            z_copy(here, zz, up).wait_send()
            ua_copy(uplace(zz, c), zz, up).wait_send()
            ub_copy(zz, up).wait_send()
            l_copy(zz, up).wait_send()

        along(zz, sent)
        for n in range(sides):
            for m in range(parts):
                side_copy(here, zz, n, m).wait_send()
        if relay:
            for n in range(2):
                diag_copy(zz, n).wait_send()
        for n, hh in enumerate(everyone):
            if relay and 1 <= n <= 2:
                for m in range(2):
                    mate_copy(zz, hh, m, piece).wait_send()
            else:
                mate_copy(zz, hh).wait_send()
        swap(zz * 2).wait_send()
        swap(zz * 2 + 1).wait_send()
        l_mate(zz, c).wait_send()
        return 0

    lax.fori_loop(0, nz, drain, 0)
    mate_up.wait_send()


def store(a_ref, b_ref, c_ref, x_ref, y_ref, z_ref, sems):
    ends = ((a_ref, x_ref), (b_ref, y_ref), (c_ref, z_ref))
    copies = [pltpu.make_async_copy(src, dst, sems.at[n]) for n, (src, dst) in enumerate(ends)]
    for copy in copies:
        copy.start()
    for copy in copies:
        copy.wait()


def local(n_seq, nh, tokens, w_query, w_key, w_value, upstream, log_decay, segment):
    nz = n_seq // 2
    rows, feat = tokens.shape
    total, depth = rows * n_seq, feat * nh
    heads = w_query.shape[1] // HEAD // 2
    width = heads * HEAD
    reach = total // 4 // rows
    parts = 2 if nh == 4 else 1
    slots = 2 if nz <= 4 else nz
    decay = jnp.zeros((max(8, 2 * heads), rows), jnp.float32).at[: 2 * heads].set(log_decay.T)
    seg = segment.reshape(n_seq, rows)
    kind = tokens.dtype
    dma = pltpu.SemaphoreType.DMA
    vmem = pl.BlockSpec(memory_space=pltpu.VMEM)
    hbm = pl.BlockSpec(memory_space=pl.ANY)
    f32 = jnp.float32
    square = (HEAD, HEAD)
    padded = n_seq + 2 * reach
    out_rows = depth // n_seq
    grads = pl.pallas_call(
        functools.partial(kernel, nz, nh, heads, reach),
        out_shape=[pltpu.VMEM((out_rows, 2 * width), kind)] * 3,
        in_specs=[hbm] * 7,
        out_specs=[vmem] * 3,
        scratch_shapes=[
            pltpu.VMEM((total, depth), kind),
            pltpu.VMEM((total, width), kind),
            pltpu.VMEM((n_seq,) + decay.shape, f32),
            pltpu.VMEM(seg.shape, seg.dtype),
            pltpu.VMEM((depth, 3 * width), kind),
        ]
        + [pltpu.VMEM((total, width), kind)] * 3
        + [pltpu.VMEM((2, 2 * rows, 3 * width), f32)]
        + [pltpu.VMEM((heads, n_seq) + square, f32)] * 3
        + [pltpu.VMEM((heads, padded, 8, HEAD), f32)]
        + [pltpu.VMEM((heads, padded) + square, kind)] * 2
        + [
            pltpu.VMEM((2, total, 3 * width), kind),
            pltpu.VMEM((slots * 2 * rows, 3 * width), f32),
            pltpu.VMEM((out_rows, total), kind),
            pltpu.VMEM((2, out_rows, 3 * width), f32),
        ]
        + [dma((2, nz)), dma((nz,))] * 3
        + [dma((nh - 1, parts, nz))] * 2
        + [dma((2, nz))] * 2
        + [dma((nz, nh, parts))] * 2
        + [dma((1,))] * 2
        + [dma((n_seq,))] * 2
        + [dma((nz,))] * 2
        + [dma((2, nz)), dma((nz,))]
        + [dma((4,)), dma((nh, 3))],
        compiler_params=pltpu.CompilerParams(collective_id=0, has_side_effects=True, vmem_limit_bytes=VMEM_BYTES),
    )(tokens, upstream, decay, seg, w_query, w_key, w_value)
    return tuple(pl.pallas_call(
        store,
        out_shape=[jax.ShapeDtypeStruct((out_rows, 2 * width), kind)] * 3,
        in_specs=[vmem] * 3,
        out_specs=[hbm] * 3,
        scratch_shapes=[dma((3,))],
    )(*[pltpu.with_memory_space_constraint(grad, pltpu.VMEM) for grad in grads]))


def solution(mesh):
    placed = (P("seq", "head"), P(None, "head"), P(None, "head"), P(None, "head"), P("seq", "head"), P("seq", "head"), P())
    return jax.shard_map(
        functools.partial(local, mesh.shape["seq"], mesh.shape["head"]),
        mesh=mesh,
        in_specs=placed,
        out_specs=(P("seq", "head"),) * 3,
        check_vma=False,
    )
```

time: 60.8 us -> 52.9 us (0.87)
  the two profiles are of different devices: /device:TPU:9 before, /device:TPU:0 now
where the time goes in v1:
time: 52.9 us; the launch traced here: 52.7 us
  Pallas kernels  52.1 us (98%)
  between operations  0.64 us (1%)
    pallas_call x1, Pallas kernels, local(): pl.pallas_call(functools.partial(kernel, nz, nh, heads, reach), out_shape...  50.4 us
    pallas_call x1, Pallas kernels, local(): pl.pallas_call(store, out_shape=[jax.ShapeDtypeStruct((out_rows, 2 * widt...  1.69 us

profile of v1, /device:TPU:0, one launch (start us, length us, event | category | flops | bytes accessed | tf_op | source)
XLA Modules:
  0.0 52.7 jit_solution(18104121950052022986)
XLA Ops:
  0.6 50.4 %shard_map.99 = (bf16[512,1024]{1,0:T(8,128)(2,1)S(1)}, bf16[512,1024]{1,0:T(8,128)(2,1)S(1)}, bf16[512,1024]{1,0:T(8,128)(2,1)S(1)}) custom-call(bf16[128,1024]{1,0:T(8,128)(2,1)} %tok_ref.1, bf16[128,1024]{1,0:T(8,128)(2,1)} %up_ref.1, f32[8,128]{1,0:T(8,128)} %bitcast.2, s32[8,128]{1,0:T(8,128)} %bitcast.3, bf16[4096,1024]{1,0:T(8,128)(2,1)} %wq_ref.1, ...), custom_call_target="tpu_custom_call" | custom-call | tf_op jit(solution)/shard_map/pallas_call | solution.py:563
  51.0 1.7 %shard_map.100 = (bf16[512,1024]{1,0:T(8,128)(2,1)}, bf16[512,1024]{1,0:T(8,128)(2,1)}, bf16[512,1024]{1,0:T(8,128)(2,1)}) custom-call(bf16[512,1024]{1,0:T(8,128)(2,1)S(1)} %get-tuple-element.26.a_ref, bf16[512,1024]{1,0:T(8,128)(2,1)S(1)} %get-tuple-element.27.b_ref, bf16[512,1024]{1,0:T(8,128)(2,1)S(1)} %get-tuple-element.28.c_ref), custom_call_target="tpu_custom_call" | custom-call | tf_op jit(solution)/shard_map/pallas_call | solution.py:597
